TPU v7x, 512 devices: a whole 4x4x16 slice. The times are simulated.
512 devices in a mesh: client: 4 (over z_hi), expert: 16 (over y, x), shard: 8 (over z_lo, core).
Axes of the slice: x: 4, y: 4, z: 16 (z_hi: 4, z_lo: 4; z = z_hi * 4 + z_lo), core: 2. Of those that a mesh axis runs over, the one named last changes fastest.
Arguments:
- tokens: bfloat16 [4, 2048, 2048], P('client', 'expert'), may hold values from -6 to 6
- target: bfloat16 [4, 2048, 2048], P('client', 'expert'), may hold values from -6 to 6
- routes: int32 [4, 2048, 2], P('client', 'expert'), may hold values from 0 to 7, all different within a row; in each aligned block of 128 rows (0 to 127, 128 to 255, ..., all dimensions but the last counted through in order) at most 32 rows name the same one
- gate_weights: float32 [4, 2048, 2], P('client', 'expert'), may hold values from 0.1 to 1
- counts: int32 [4], replicated, may hold values from 512 to 2048
- gate_proj: bfloat16 [57344, 2048], P(('expert', 'shard'), 'client'), may hold values from -0.125 to 0.125
- up_proj: bfloat16 [57344, 2048], P(('expert', 'shard'), 'client'), may hold values from -0.125 to 0.125
- down_proj: bfloat16 [57344, 2048], P(('expert', 'shard'), 'client'), may hold values from -0.0625 to 0.0625
- correction: bfloat16 [4, 57344, 2048], P('client', ('expert', 'shard')), may hold values from -6 to 6
Outputs:
- pseudo_gradient: float32 [57344, 2048], P(('expert', 'shard'), 'client')
Inputs may be any that keep to these rules, and one draw needn't show every extreme that they name: `routes`: in each aligned block of 128 rows of a client, every expert is named by exactly 32 rows; the 2 ids of a row differ.
All inputs are finite; a program needn't handle non-finite values.
Results may differ from a plain program's by a relative error of at most 0.015.
Values may be sent and summed in bfloat16 or wider, within the bound.
No kernel may reach another device: no remote copies, remote signals or barrier semaphores. Data moves between devices by JAX's collectives and lax.ppermute only.
A program may use at most 64 MiB of HBM per device.

v0:
```python
import jax
import jax.numpy as jnp
from jax import lax
from jax.sharding import PartitionSpec as P

FF = 7168
EXPERTS = 8
LOCAL_STEPS = 2


def sent_together(arrays, axis, dim, along):
    ends, at = ([], 0)
    for a in arrays[:-1]:
        at += a.shape[along]
        ends.append(at)
    both = jnp.concatenate(arrays, axis=along)
    return tuple(jnp.split(lax.all_gather(both, axis, axis=dim, tiled=True), ends, axis=along))


def in_blocks(x, dim, peers):
    shape = x.shape
    parts = x.reshape(*shape[:dim], peers, shape[dim] // peers, *shape[dim + 1 :])
    return jnp.moveaxis(parts, dim, 0)


def sum_at_owner(x, axis, dim):
    peers = lax.axis_size(axis)
    parts = lax.all_to_all(in_blocks(x, dim, peers), axis, 0, 0, tiled=True)
    return jnp.sum(parts.astype(jnp.float32), axis=0)


def local(tokens, target, routes, gate_weights, counts, gate_proj, up_proj, down_proj, correction):
    expert_count = lax.axis_size("expert")
    shard_count = lax.axis_size("shard")
    client_count = lax.axis_size("client")
    expert_index = lax.axis_index("expert")
    shard_index = lax.axis_index("shard")
    client_index = lax.axis_index("client")
    unit_count = down_proj.shape[0]
    token_count = tokens.shape[1]
    top_count = routes.shape[2]
    feature_width = tokens.shape[2]
    capacity = token_count * top_count // EXPERTS
    per_index = shard_count * unit_count
    hosted = max(1, per_index // FF)
    copies = max(1, FF // per_index)
    own_expert = (expert_index * shard_count + shard_index) * unit_count // FF
    first_expert = expert_index * per_index // FF
    share_width = feature_width // shard_count
    flat_routes = routes[0].reshape(-1)
    onehot = (flat_routes[:, None] == jnp.arange(EXPERTS, dtype=jnp.int32)[None, :]).astype(
        jnp.int32
    )
    rank_of = jnp.sum((jnp.cumsum(onehot, axis=0) - 1) * onehot, axis=1)
    slot_of = flat_routes * capacity + rank_of
    source_of = (
        jnp.zeros((EXPERTS * capacity,), jnp.int32)
        .at[slot_of]
        .set(jnp.arange(token_count * top_count, dtype=jnp.int32))
    )

    def arrange(slots, width):
        blocks = slots.reshape(EXPERTS, capacity, width)
        return jnp.repeat(blocks, copies, axis=0)

    def own_of(arrived):
        return arrived.reshape(expert_count * capacity, feature_width)

    token_slots = jnp.take(tokens[0], source_of // top_count, axis=0)
    send_blocks = arrange(token_slots, feature_width)
    send_arrived = lax.all_to_all(send_blocks, "expert", split_axis=0, concat_axis=0, tiled=True)
    features = own_of(send_arrived)
    contract = (((1,), (1,)), ((), ()))
    full_gate, full_up = sent_together((gate_proj, up_proj), "client", 1, 0)
    gate_pre = lax.dot_general(features, full_gate, contract, preferred_element_type=jnp.float32)
    up_pre = lax.dot_general(features, full_up, contract, preferred_element_type=jnp.float32)
    hidden = (jax.nn.silu(gate_pre) * up_pre).astype(jnp.bfloat16)
    down_full = lax.all_gather(down_proj, "client", axis=1, tiled=True)
    control = correction[0]
    grad_sum = None
    gate_rows = gate_weights[0]
    positions = expert_index * token_count + jnp.arange(token_count, dtype=jnp.int32)
    live_rows = (positions < counts[client_index]).astype(jnp.float32)
    sender_group = (
        (jnp.arange(expert_count, dtype=jnp.int32) * per_index // FF)[:, None]
        + jnp.arange(hosted, dtype=jnp.int32)[None, :]
    ).reshape(-1)
    group_pick = (jnp.arange(EXPERTS, dtype=jnp.int32)[:, None] == sender_group[None, :]).astype(
        jnp.float32
    )
    hosted_mask = (jnp.arange(hosted, dtype=jnp.int32) == own_expert - first_expert).astype(
        jnp.float32
    )
    target_rows = target[0].astype(jnp.float32)
    step_size = 2.0 / FF
    for step_number in range(LOCAL_STEPS):
        if step_number == 0:
            current = down_full
        else:
            current = (
                down_full.astype(jnp.float32)
                - step_size * (grad_sum + float(step_number) * control.astype(jnp.float32))
            ).astype(jnp.bfloat16)
        partial_value = jnp.dot(hidden, current, preferred_element_type=jnp.float32).astype(
            jnp.bfloat16
        )
        placed = (
            partial_value.astype(jnp.float32).reshape(expert_count, 1, capacity, feature_width)
            * hosted_mask[None, :, None, None]
        )
        placed = placed.reshape(expert_count, hosted * capacity, feature_width)
        shared = sum_at_owner(placed.astype(jnp.bfloat16), "shard", 2)
        returned = lax.all_to_all(
            shared.astype(jnp.bfloat16), "expert", split_axis=0, concat_axis=0, tiled=True
        ).astype(shared.dtype)
        slot_sums = jnp.einsum("ej,jcd->ecd", group_pick, returned, precision=lax.Precision.HIGHEST)
        slot_sums = slot_sums.reshape(EXPERTS * capacity, share_width)
        picked = jnp.take(slot_sums, slot_of, axis=0).reshape(token_count, top_count, share_width)
        output = jnp.sum(gate_rows[:, :, None] * picked, axis=1)
        target_share = lax.dynamic_slice_in_dim(
            target_rows, shard_index * share_width, share_width, 1
        )
        residual = live_rows[:, None] * (output - target_share)
        cotangent = (gate_rows[:, :, None] * residual[:, None, :]).astype(jnp.bfloat16)
        cotangent = cotangent.reshape(token_count * top_count, share_width)
        blocks = arrange(jnp.take(cotangent, source_of, axis=0), share_width)
        arrived = lax.all_to_all(blocks, "expert", split_axis=0, concat_axis=0, tiled=True)
        arrived = own_of(lax.all_gather(arrived, "shard", axis=2, tiled=True))
        gradient = lax.dot_general(
            hidden, arrived, (((0,), (0,)), ((), ())), preferred_element_type=jnp.float32
        )
        if step_number == 0:
            grad_sum = gradient
        else:
            grad_sum = grad_sum + gradient
    weight_share = counts[client_index].astype(jnp.float32) / jnp.sum(counts).astype(jnp.float32)
    client_term = (weight_share * (grad_sum / LOCAL_STEPS + control.astype(jnp.float32))).astype(
        jnp.bfloat16
    )
    client_term = client_term.reshape(unit_count, client_count, feature_width // client_count)
    received = lax.all_to_all(client_term, "client", split_axis=1, concat_axis=1, tiled=True)
    return jnp.sum(received.astype(jnp.float32), axis=1)


def solution(mesh):
    return jax.shard_map(
        local,
        mesh=mesh,
        in_specs=(
            P("client", "expert", None),
            P("client", "expert", None),
            P("client", "expert", None),
            P("client", "expert", None),
            P(),
            P(("expert", "shard"), "client"),
            P(("expert", "shard"), "client"),
            P(("expert", "shard"), "client"),
            P("client", ("expert", "shard"), None),
        ),
        out_specs=P(("expert", "shard"), "client"),
        check_vma=False,
    )
```

profile of v0, /device:TPU:1, one launch (start us, length us, event | category | flops | bytes accessed | tf_op | source)
XLA Modules:
  0.0 610.1 jit_solution(7069356703528246979)
XLA Ops:
  6.5 2.2 pad_maximum_fusion
  10.4 1.4 scatter_custom_fusion
  13.5 1.6 broadcast_in_dim.54
  15.1 7.6 %all-to-all-start = ((bf16[16,32,2048]{2,1,0:T(8,128)(2,1)}), bf16[16,32,2048]{2,1,0:T(8,128)(2,1)S(1)}, u32[]{:S(2)}, u32[]{:S(2)}) async-start(bf16[16,32,2048]{2,1,0:T(8,128)(2,1)} %bitcast.7), calls=%async_computation | async-start | bytes 4194304 | tf_op jit(solution)/shard_map/all_to_all | solution.py:71
  23.5 24.8 %all-to-all-done = bf16[16,32,2048]{2,1,0:T(8,128)(2,1)S(1)} async-done(((bf16[16,32,2048]{2,1,0:T(8,128)(2,1)}), bf16[16,32,2048]{2,1,0:T(8,128)(2,1)S(1)}, u32[]{:S(2)}, u32[]{:S(2)}) %all-to-all-start) | async-done | bytes 2097184 | tf_op jit(solution)/shard_map/all_to_all | solution.py:71
  48.3 113.6 %all-gather.5.cloned.1.call-done = bf16[896,2048]{1,0:T(8,128)(2,1)} async-done(((bf16[896,512]{1,0:T(8,128)(2,1)}), bf16[896,2048]{1,0:T(8,128)(2,1)}) %all-gather.5.cloned.1.call-update) | async-done | bytes 3670032 | tf_op jit(solution)/shard_map/all_gather | solution.py:17
  161.9 2.8 fusion.8
  165.9 77.4 %all-gather.7.cloned.1.call-done = bf16[448,2048]{1,0:T(8,128)(2,1)} async-done(((bf16[448,512]{1,0:T(8,128)(2,1)}), bf16[448,2048]{1,0:T(8,128)(2,1)}) %all-gather.7.cloned.1.call-update) | async-done | bytes 1835024 | tf_op jit(solution)/shard_map/all_gather | solution.py:78
  243.4 2.8 multiply_convert_fusion.1
  246.9 1.8 copy.45
  248.7 4.9 all-to-all-start.1
  254.3 47.4 %all-to-all-done.1 = bf16[8,16,32,256]{3,2,1,0:T(8,128)(2,1)S(1)} async-done(((bf16[8,16,32,256]{3,2,1,0:T(8,128)(2,1)}), bf16[8,16,32,256]{3,2,1,0:T(8,128)(2,1)S(1)}, u32[]{:S(2)}, u32[]{:S(2)}) %all-to-all-start.1) | async-done | bytes 2097184 | tf_op jit(solution)/shard_map/all_to_all | solution.py:28
  302.8 7.1 %all-to-all-start.2 = ((bf16[16,32,256]{2,1,0:T(8,128)(2,1)}), bf16[16,32,256]{2,1,0:T(8,128)(2,1)S(1)}, u32[]{:S(2)}, u32[]{:S(2)}) async-start(bf16[16,32,256]{2,1,0:T(8,128)(2,1)} %reduce_sum.74), calls=%async_computation.2 | async-start | bytes 524288 | tf_op jit(solution)/shard_map/all_to_all | solution.py:113
  311.1 6.5 %all-to-all-done.2 = bf16[16,32,256]{2,1,0:T(8,128)(2,1)S(1)} async-done(((bf16[16,32,256]{2,1,0:T(8,128)(2,1)}), bf16[16,32,256]{2,1,0:T(8,128)(2,1)S(1)}, u32[]{:S(2)}, u32[]{:S(2)}) %all-to-all-start.2) | async-done | bytes 262176 | tf_op jit(solution)/shard_map/all_to_all | solution.py:113
  322.2 10.8 %all_to_all.40 = bf16[16,32,256]{2,1,0:T(8,128)(2,1)} all-to-all(bf16[16,32,256]{2,1,0:T(8,128)(2,1)S(1)} %bitcast.81), channel_id=1, replica_groups=mesh['client'=4,'expert'=16,'shard'=8] {'expert'}, dimensions={0} | all-to-all | bytes 524288 | tf_op jit(solution)/shard_map/all_to_all | solution.py:127
  333.3 40.3 %all-gather.9.cloned.1.call-done = bf16[16,32,2048]{2,1,0:T(8,128)(2,1)} async-done(((bf16[16,32,256]{2,1,0:T(8,128)(2,1)}), bf16[16,32,2048]{2,1,0:T(8,128)(2,1)}) %all-gather.9.cloned.1.call-update) | async-done | bytes 2097168 | tf_op jit(solution)/shard_map/all_gather | solution.py:128
  373.5 2.9 fusion.34
  379.4 51.2 %all_to_all.41 = bf16[8,16,32,256]{3,2,1,0:T(8,128)(2,1)} all-to-all(bf16[8,16,32,256]{3,2,1,0:T(8,128)(2,1)S(1)} %bitcast.73), channel_id=1, replica_groups=mesh['client'=4,'expert'=16,'shard'=8] {'shard'}, dimensions={0} | all-to-all | bytes 4194304 | tf_op jit(solution)/shard_map/all_to_all | solution.py:28
  430.6 2.0 reduce_sum.76
  432.6 14.0 %all_to_all.42 = bf16[16,32,256]{2,1,0:T(8,128)(2,1)S(1)} all-to-all(bf16[16,32,256]{2,1,0:T(8,128)(2,1)S(1)} %reduce_sum.76), channel_id=1, replica_groups=mesh['client'=4,'expert'=16,'shard'=8] {'expert'}, dimensions={0} | all-to-all | bytes 524288 | tf_op jit(solution)/shard_map/all_to_all | solution.py:113
  451.2 10.8 %all_to_all.43 = bf16[16,32,256]{2,1,0:T(8,128)(2,1)} all-to-all(bf16[16,32,256]{2,1,0:T(8,128)(2,1)S(1)} %bitcast.82), channel_id=1, replica_groups=mesh['client'=4,'expert'=16,'shard'=8] {'expert'}, dimensions={0} | all-to-all | bytes 524288 | tf_op jit(solution)/shard_map/all_to_all | solution.py:127
  464.1 40.1 %all-gather.11.cloned.1.call-done = bf16[16,32,2048]{2,1,0:T(8,128)(2,1)} async-done(((bf16[16,32,256]{2,1,0:T(8,128)(2,1)}), bf16[16,32,2048]{2,1,0:T(8,128)(2,1)}) %all-gather.11.cloned.1.call-update) | async-done | bytes 2097168 | tf_op jit(solution)/shard_map/all_gather | solution.py:128
  504.2 4.0 fusion.4
  508.4 94.0 %all_to_all.44 = bf16[448,4,512]{2,0,1:T(8,128)(2,1)S(1)} all-to-all(bf16[448,4,512]{2,0,1:T(8,128)(2,1)S(1)} %bitcast.74), channel_id=1, replica_groups=mesh['client'=4,'expert'=16,'shard'=8] {'client'}, dimensions={1} | all-to-all | bytes 3670016 | tf_op jit(solution)/shard_map/all_to_all | solution.py:141
  (88 shorter events, 23.0 us)
Async XLA Ops:
  6.5 5.4 copy-start
  6.5 2.2 copy-start.5
  6.5 155.3 %all-gather.5.cloned.1.call-start = ((), (), s32[]{:S(2)}) async-start(), calls=%async_computation.8 | async-start | bytes 4587520 | tf_op jit(solution)/shard_map/all_gather | solution.py:17
  15.1 33.2 %all-to-all-start = ((bf16[16,32,2048]{2,1,0:T(8,128)(2,1)}), bf16[16,32,2048]{2,1,0:T(8,128)(2,1)S(1)}, u32[]{:S(2)}, u32[]{:S(2)}) async-start(bf16[16,32,2048]{2,1,0:T(8,128)(2,1)} %bitcast.7), calls=%async_computation | async-start | bytes 4194304 | tf_op jit(solution)/shard_map/all_to_all | solution.py:71
  22.7 220.7 %all-gather.7.cloned.1.call-start = ((), (), s32[]{:S(2)}) async-start(), calls=%async_computation.9 | async-start | bytes 2293760 | tf_op jit(solution)/shard_map/all_gather | solution.py:78
  161.9 2.8 copy-start.6
  248.7 4.9 copy-start.7
  248.7 53.0 %all-to-all-start.1 = ((bf16[8,16,32,256]{3,2,1,0:T(8,128)(2,1)}), bf16[8,16,32,256]{3,2,1,0:T(8,128)(2,1)S(1)}, u32[]{:S(2)}, u32[]{:S(2)}) async-start(bf16[8,16,32,256]{3,2,1,0:T(8,128)(2,1)} %bitcast.70), calls=%async_computation.1 | async-start | bytes 4194304 | tf_op jit(solution)/shard_map/all_to_all | solution.py:28
  253.6 57.1 %copy-start.4 = (f32[1,128,2]{1,2,0:T(2,128)S(1)}, f32[1,128,2]{1,2,0:T(2,128)}, u32[]{:S(2)}) copy-start(f32[1,128,2]{1,2,0:T(2,128)} %param.16) | copy-start | bytes 3076
  302.8 14.8 %all-to-all-start.2 = ((bf16[16,32,256]{2,1,0:T(8,128)(2,1)}), bf16[16,32,256]{2,1,0:T(8,128)(2,1)S(1)}, u32[]{:S(2)}, u32[]{:S(2)}) async-start(bf16[16,32,256]{2,1,0:T(8,128)(2,1)} %reduce_sum.74), calls=%async_computation.2 | async-start | bytes 524288 | tf_op jit(solution)/shard_map/all_to_all | solution.py:113
  309.9 63.6 %all-gather.9.cloned.1.call-start = ((), (), s32[]{:S(2)}) async-start(), calls=%async_computation.10 | async-start | bytes 2359296 | tf_op jit(solution)/shard_map/all_gather | solution.py:128
  333.1 171.1 %all-gather.11.cloned.1.call-start = ((), (), s32[]{:S(2)}) async-start(), calls=%async_computation.11 | async-start | bytes 2359296 | tf_op jit(solution)/shard_map/all_gather | solution.py:128
  373.5 2.9 copy-start.2
  373.5 2.9 copy-start.3
  376.4 1.8 copy-start.1
Sparse Core Ops, SparseCore 0:
  9.4 152.4 all-gather.4
  164.0 79.3 all-gather.6
  333.2 40.3 all-gather.8
  462.2 41.9 all-gather.10
where the time goes:
time: 611 us; the launch traced here: 610 us
  waiting for transfers between devices  351 us (57%)
  blocking collectives  181 us (30%)
  starting transfers between devices  19.9 us (3%)
  local copies, waits for them, and re-layouts  15.9 us (3%)
  matrix products  15.6 us (3%)
  between operations  15 us (2%)
  other arithmetic  12 us (2%)
    all_gather x1, waiting for transfers between devices, sent_together(): lax.all_gather(both, axis, axis=dim, tiled=True)  114 us
    all_to_all x1, blocking collectives, local(): lax.all_to_all(client_term, 'client', split_axis=1, concat_axis=1, tiled=...  94 us
    all_gather x2, waiting for transfers between devices, local(): arrived = own_of(lax.all_gather(arrived, 'shard', axis=2, tiled=True))  80.4 us
    all_gather x1, waiting for transfers between devices, local(): down_full = lax.all_gather(down_proj, 'client', axis=1, tiled=True)  77.4 us
    all_to_all x1, blocking collectives, sum_at_owner(): parts = lax.all_to_all(in_blocks(x, dim, peers), axis, 0, 0, tiled=True)  51.2 us
    all_to_all x1, waiting for transfers between devices, sum_at_owner(): parts = lax.all_to_all(in_blocks(x, dim, peers), axis, 0, 0, tiled=True)  47.4 us
    all_to_all x1, waiting for transfers between devices, local(): lax.all_to_all(send_blocks, 'expert', split_axis=0, concat_axis=0, tiled=...  24.8 us
    all_to_all x2, blocking collectives, local(): lax.all_to_all(blocks, 'expert', split_axis=0, concat_axis=0, tiled=True)  21.6 us
  transfers between devices with their start and end apart: 7, of which 7 were waited for; matrix products, arithmetic and copies ran while one was open for 2% of the time, Pallas kernels for 0%

commit v1 on v0

--- a/solution.py
+++ b/solution.py
@@ -1,3 +1,4 @@
+import functools
 import jax
 import jax.numpy as jnp
 from jax import lax
@@ -6,6 +7,21 @@
 FF = 7168
 EXPERTS = 8
 LOCAL_STEPS = 2
+
+
+def change_thing(s0, comm_axis, in_dim):
+    return jnp.concatenate(
+        lax.all_to_all(
+            jnp.stack(lax.axis_size(comm_axis) * [s0], axis=0),
+            axis_name=comm_axis,
+            split_axis=0,
+            concat_axis=0,
+        ),
+        axis=in_dim,
+    )
+
+
+_derive_classes = functools.partial(change_thing, comm_axis="shard", in_dim=2)
 
 
 def sent_together(arrays, axis, dim, along):
@@ -125,7 +141,7 @@
         cotangent = cotangent.reshape(token_count * top_count, share_width)
         blocks = arrange(jnp.take(cotangent, source_of, axis=0), share_width)
         arrived = lax.all_to_all(blocks, "expert", split_axis=0, concat_axis=0, tiled=True)
-        arrived = own_of(lax.all_gather(arrived, "shard", axis=2, tiled=True))
+        arrived = own_of(_derive_classes(arrived))
         gradient = lax.dot_general(
             hidden, arrived, (((0,), (0,)), ((), ())), preferred_element_type=jnp.float32
         )

time: 611 us -> 640 us (1.047)
  blocking collectives: 181 us -> 228 us
  waiting for transfers between devices: 351 us -> 317 us
  local copies, waits for them, and re-layouts: 15.9 us -> 25.8 us
  starting transfers between devices: 19.9 us -> 27.5 us
    all_gather x2 -> x0, waiting for transfers between devices: 80.4 us -> none  [local(): arrived = own_of(lax.all_gather(arrived, 'shard', axis=2, tiled=True))]
    all_to_all x0 -> x1, blocking collectives: none -> 54.1 us  [change_thing(): lax.all_to_all(jnp.stack(lax.axis_size(comm_axis) * [s0], axis=0), axis_n...]
    all_to_all x0 -> x1, waiting for transfers between devices: none -> 46.3 us  [change_thing(): lax.all_to_all(jnp.stack(lax.axis_size(comm_axis) * [s0], axis=0), axis_n...]
    all_to_all x0 -> x1, starting transfers between devices: none -> 7.82 us  [change_thing(): lax.all_to_all(jnp.stack(lax.axis_size(comm_axis) * [s0], axis=0), axis_n...]
  transfers between devices with their start and end apart: 7 -> 6, of which waited for: 7 -> 6; matrix products, arithmetic and copies ran while one was open for 2% -> 2% of each run, Pallas kernels for 0% -> 0%
where the time goes in v1:
time: 640 us; the launch traced here: 637 us
  waiting for transfers between devices  317 us (50%)
  blocking collectives  228 us (36%)
  starting transfers between devices  27.5 us (4%)
  local copies, waits for them, and re-layouts  25.8 us (4%)
  between operations  15.2 us (2%)
  other arithmetic  11.9 us (2%)
  matrix products  11.3 us (2%)
    all_gather x1, waiting for transfers between devices, sent_together(): lax.all_gather(both, axis, axis=dim, tiled=True)  114 us
    all_to_all x1, blocking collectives, local(): lax.all_to_all(client_term, 'client', split_axis=1, concat_axis=1, tiled=...  91.1 us
    all_gather x1, waiting for transfers between devices, local(): down_full = lax.all_gather(down_proj, 'client', axis=1, tiled=True)  77.4 us
    all_to_all x1, blocking collectives, change_thing(): lax.all_to_all(jnp.stack(lax.axis_size(comm_axis) * [s0], axis=0), axis_n...  54.1 us
    all_to_all x1, blocking collectives, sum_at_owner(): parts = lax.all_to_all(in_blocks(x, dim, peers), axis, 0, 0, tiled=True)  52.2 us
    all_to_all x1, waiting for transfers between devices, sum_at_owner(): parts = lax.all_to_all(in_blocks(x, dim, peers), axis, 0, 0, tiled=True)  47.4 us
    all_to_all x1, waiting for transfers between devices, change_thing(): lax.all_to_all(jnp.stack(lax.axis_size(comm_axis) * [s0], axis=0), axis_n...  46.3 us
    all_to_all x1, waiting for transfers between devices, local(): lax.all_to_all(send_blocks, 'expert', split_axis=0, concat_axis=0, tiled=...  24.8 us
  transfers between devices with their start and end apart: 6, of which 6 were waited for; matrix products, arithmetic and copies ran while one was open for 2% of the time, Pallas kernels for 0%

profile of v1, /device:TPU:1, one launch (start us, length us, event | category | flops | bytes accessed | tf_op | source)
XLA Modules:
  0.0 636.8 jit_solution(3160299699553065373)
XLA Ops:
  6.5 2.2 pad_maximum_fusion
  13.5 1.6 broadcast_in_dim.54
  15.1 7.6 %all-to-all-start = ((bf16[16,32,2048]{2,1,0:T(8,128)(2,1)}), bf16[16,32,2048]{2,1,0:T(8,128)(2,1)S(1)}, u32[]{:S(2)}, u32[]{:S(2)}) async-start(bf16[16,32,2048]{2,1,0:T(8,128)(2,1)} %bitcast.7), calls=%async_computation | async-start | bytes 4194304 | tf_op jit(solution)/shard_map/all_to_all | solution.py:87
  23.5 24.8 %all-to-all-done = bf16[16,32,2048]{2,1,0:T(8,128)(2,1)S(1)} async-done(((bf16[16,32,2048]{2,1,0:T(8,128)(2,1)}), bf16[16,32,2048]{2,1,0:T(8,128)(2,1)S(1)}, u32[]{:S(2)}, u32[]{:S(2)}) %all-to-all-start) | async-done | bytes 2097184 | tf_op jit(solution)/shard_map/all_to_all | solution.py:87
  48.3 113.6 %all-gather.3.cloned.1.call-done = bf16[896,2048]{1,0:T(8,128)(2,1)} async-done(((bf16[896,512]{1,0:T(8,128)(2,1)}), bf16[896,2048]{1,0:T(8,128)(2,1)}) %all-gather.3.cloned.1.call-update) | async-done | bytes 3670032 | tf_op jit(solution)/shard_map/all_gather | solution.py:33
  161.9 2.8 fusion.8
  165.9 77.4 %all-gather.5.cloned.1.call-done = bf16[448,2048]{1,0:T(8,128)(2,1)} async-done(((bf16[448,512]{1,0:T(8,128)(2,1)}), bf16[448,2048]{1,0:T(8,128)(2,1)}) %all-gather.5.cloned.1.call-update) | async-done | bytes 1835024 | tf_op jit(solution)/shard_map/all_gather | solution.py:94
  243.4 2.8 multiply_convert_fusion.1
  246.9 1.8 copy.49
  248.7 4.9 all-to-all-start.1
  254.3 47.4 %all-to-all-done.1 = bf16[8,16,32,256]{3,2,1,0:T(8,128)(2,1)S(1)} async-done(((bf16[8,16,32,256]{3,2,1,0:T(8,128)(2,1)}), bf16[8,16,32,256]{3,2,1,0:T(8,128)(2,1)S(1)}, u32[]{:S(2)}, u32[]{:S(2)}) %all-to-all-start.1) | async-done | bytes 2097184 | tf_op jit(solution)/shard_map/all_to_all | solution.py:44
  302.8 7.1 %all-to-all-start.2 = ((bf16[16,32,256]{2,1,0:T(8,128)(2,1)}), bf16[16,32,256]{2,1,0:T(8,128)(2,1)S(1)}, u32[]{:S(2)}, u32[]{:S(2)}) async-start(bf16[16,32,256]{2,1,0:T(8,128)(2,1)} %reduce_sum.74), calls=%async_computation.2 | async-start | bytes 524288 | tf_op jit(solution)/shard_map/all_to_all | solution.py:129
  311.0 6.7 %all-to-all-done.2 = bf16[16,32,256]{2,1,0:T(8,128)(2,1)S(1)} async-done(((bf16[16,32,256]{2,1,0:T(8,128)(2,1)}), bf16[16,32,256]{2,1,0:T(8,128)(2,1)S(1)}, u32[]{:S(2)}, u32[]{:S(2)}) %all-to-all-start.2) | async-done | bytes 262176 | tf_op jit(solution)/shard_map/all_to_all | solution.py:129
  322.2 10.3 %all_to_all.50 = bf16[16,32,256]{2,1,0:T(8,128)(2,1)S(1)} all-to-all(bf16[16,32,256]{2,1,0:T(8,128)(2,1)S(1)} %bitcast.90), channel_id=1, replica_groups=mesh['client'=4,'expert'=16,'shard'=8] {'expert'}, dimensions={0} | all-to-all | bytes 524288 | tf_op jit(solution)/shard_map/all_to_all | solution.py:143
  332.8 54.1 %all_to_all.51 = bf16[8,16,32,256]{3,2,1,0:T(8,128)(2,1)S(1)} all-to-all(bf16[8,16,32,256]{3,2,1,0:T(8,128)(2,1)S(1)} %stack.4), channel_id=1, replica_groups=mesh['client'=4,'expert'=16,'shard'=8] {'shard'}, dimensions={0} | all-to-all | bytes 4194304 | tf_op jit(solution)/shard_map/all_to_all | solution.py:14
  394.0 52.2 %all_to_all.52 = bf16[8,16,32,256]{3,2,1,0:T(8,128)(2,1)} all-to-all(bf16[8,16,32,256]{3,2,1,0:T(8,128)(2,1)S(1)} %bitcast.83), channel_id=1, replica_groups=mesh['client'=4,'expert'=16,'shard'=8] {'shard'}, dimensions={0} | all-to-all | bytes 4194304 | tf_op jit(solution)/shard_map/all_to_all | solution.py:44
  446.2 2.0 reduce_sum.76
  448.2 10.3 %all_to_all.53 = bf16[16,32,256]{2,1,0:T(8,128)(2,1)S(1)} all-to-all(bf16[16,32,256]{2,1,0:T(8,128)(2,1)S(1)} %reduce_sum.76), channel_id=1, replica_groups=mesh['client'=4,'expert'=16,'shard'=8] {'expert'}, dimensions={0} | all-to-all | bytes 524288 | tf_op jit(solution)/shard_map/all_to_all | solution.py:129
  463.1 10.3 %all_to_all.54 = bf16[16,32,256]{2,1,0:T(8,128)(2,1)S(1)} all-to-all(bf16[16,32,256]{2,1,0:T(8,128)(2,1)S(1)} %bitcast.91), channel_id=1, replica_groups=mesh['client'=4,'expert'=16,'shard'=8] {'expert'}, dimensions={0} | all-to-all | bytes 524288 | tf_op jit(solution)/shard_map/all_to_all | solution.py:143
  473.4 1.6 stack.5
  475.0 7.8 %all-to-all-start.8 = ((bf16[8,16,32,256]{3,2,1,0:T(8,128)(2,1)}), bf16[8,16,32,256]{3,2,1,0:T(8,128)(2,1)}, u32[]{:S(2)}, u32[]{:S(2)}) async-start(bf16[8,16,32,256]{3,2,1,0:T(8,128)(2,1)} %stack.5), calls=%async_computation.8 | async-start | bytes 4194304 | tf_op jit(solution)/shard_map/all_to_all | solution.py:14
  484.8 46.3 %all-to-all-done.8 = bf16[8,16,32,256]{3,2,1,0:T(8,128)(2,1)} async-done(((bf16[8,16,32,256]{3,2,1,0:T(8,128)(2,1)}), bf16[8,16,32,256]{3,2,1,0:T(8,128)(2,1)}, u32[]{:S(2)}, u32[]{:S(2)}) %all-to-all-start.8) | async-done | bytes 2097184 | tf_op jit(solution)/shard_map/all_to_all | solution.py:14
  531.0 3.0 copy.32
  537.7 91.1 %all_to_all.55 = bf16[448,4,512]{2,0,1:T(8,128)(2,1)S(1)} all-to-all(bf16[448,4,512]{2,0,1:T(8,128)(2,1)S(1)} %bitcast.85), channel_id=1, replica_groups=mesh['client'=4,'expert'=16,'shard'=8] {'client'}, dimensions={1} | all-to-all | bytes 3670016 | tf_op jit(solution)/shard_map/all_to_all | solution.py:157
  (95 shorter events, 31.9 us)
Async XLA Ops:
  6.5 5.4 copy-start
  6.5 2.2 copy-start.7
  6.5 155.3 %all-gather.3.cloned.1.call-start = ((), (), s32[]{:S(2)}) async-start(), calls=%async_computation.10 | async-start | bytes 4587520 | tf_op jit(solution)/shard_map/all_gather | solution.py:33
  15.1 33.2 %all-to-all-start = ((bf16[16,32,2048]{2,1,0:T(8,128)(2,1)}), bf16[16,32,2048]{2,1,0:T(8,128)(2,1)S(1)}, u32[]{:S(2)}, u32[]{:S(2)}) async-start(bf16[16,32,2048]{2,1,0:T(8,128)(2,1)} %bitcast.7), calls=%async_computation | async-start | bytes 4194304 | tf_op jit(solution)/shard_map/all_to_all | solution.py:87
  22.7 220.7 %all-gather.5.cloned.1.call-start = ((), (), s32[]{:S(2)}) async-start(), calls=%async_computation.11 | async-start | bytes 2293760 | tf_op jit(solution)/shard_map/all_gather | solution.py:94
  161.9 2.8 copy-start.8
  248.7 4.9 copy-start.9
  248.7 53.0 %all-to-all-start.1 = ((bf16[8,16,32,256]{3,2,1,0:T(8,128)(2,1)}), bf16[8,16,32,256]{3,2,1,0:T(8,128)(2,1)S(1)}, u32[]{:S(2)}, u32[]{:S(2)}) async-start(bf16[8,16,32,256]{3,2,1,0:T(8,128)(2,1)} %bitcast.77), calls=%async_computation.1 | async-start | bytes 4194304 | tf_op jit(solution)/shard_map/all_to_all | solution.py:44
  253.6 57.0 %copy-start.6 = (f32[1,128,2]{1,2,0:T(2,128)S(1)}, f32[1,128,2]{1,2,0:T(2,128)}, u32[]{:S(2)}) copy-start(f32[1,128,2]{1,2,0:T(2,128)} %param.16) | copy-start | bytes 3076
  302.8 14.8 %all-to-all-start.2 = ((bf16[16,32,256]{2,1,0:T(8,128)(2,1)}), bf16[16,32,256]{2,1,0:T(8,128)(2,1)S(1)}, u32[]{:S(2)}, u32[]{:S(2)}) async-start(bf16[16,32,256]{2,1,0:T(8,128)(2,1)} %reduce_sum.74), calls=%async_computation.2 | async-start | bytes 524288 | tf_op jit(solution)/shard_map/all_to_all | solution.py:129
  389.0 1.5 copy-start.4
  389.0 2.0 copy-start.5
  391.1 1.8 copy-start.2
  475.0 56.0 %all-to-all-start.8 = ((bf16[8,16,32,256]{3,2,1,0:T(8,128)(2,1)}), bf16[8,16,32,256]{3,2,1,0:T(8,128)(2,1)}, u32[]{:S(2)}, u32[]{:S(2)}) async-start(bf16[8,16,32,256]{3,2,1,0:T(8,128)(2,1)} %stack.5), calls=%async_computation.8 | async-start | bytes 4194304 | tf_op jit(solution)/shard_map/all_to_all | solution.py:14
  534.0 2.0 copy-start.3
  537.7 92.3 %copy-start.1 = (bf16[1,128,2048]{2,1,0:T(8,128)(2,1)S(1)}, bf16[1,128,2048]{2,1,0:T(8,128)(2,1)}, u32[]{:S(2)}) copy-start(bf16[1,128,2048]{2,1,0:T(8,128)(2,1)} %param.13) | copy-start | bytes 1572868
Sparse Core Ops, SparseCore 0:
  9.4 152.4 all-gather.2
  164.0 79.3 all-gather.4
